TPU v7x, 32 devices: a whole 2x2x4 slice. The times are simulated.
32 devices in a mesh: lag: 2 (over core), space: 16 (over z, y, x).
Axes of the slice: x: 2, y: 2, z: 4, core: 2. Of those that a mesh axis runs over, the one named last changes fastest.
Arguments:
- ensemble: bfloat16 [2, 64, 65536], P('lag', None, 'space'), may hold values from -6 to 6
- obs_pert: bfloat16 [2, 64, 16384], P('lag', None, 'space'), may hold values from -6 to 6
- obs_innov: bfloat16 [2, 16384], P('lag', 'space'), may hold values from -12 to 12
- obs_rinv: bfloat16 [2, 16384], P('lag', 'space'), may hold values from 0.019897461 to 0.5
- obs_tile: int32 [2, 16384, 1], P('lag', 'space'), may hold values from 0 to 15; in each aligned block of 1024 rows (0 to 1023, 1024 to 2047, ..., all dimensions but the last counted through in order) at most 128 rows name the same one
- obs_column: int32 [2, 16384], P('lag', 'space'), may hold values from 0 to 4095
- obs_count: int32 [2, 16], P('lag', 'space'), may hold values from 512 to 1024, as said below
Outputs:
- analysis: bfloat16 [2, 64, 65536], P('lag', None, 'space')
Inputs may be any that keep to these rules, and one draw needn't show every extreme that they name: `obs_tile`: among the 1024 slots of one device at one lag, no tile is named more than 128 times. `obs_count`: slots of a device past its count are not used; in every draw some device uses all 1024.
All inputs are finite; a program needn't handle non-finite values.
Results may differ from a plain program's by a relative error of at most 0.0022.
The roundings to bfloat16 on the way count: a program that leaves them out, or rounds other values in their place, can miss the bound.
Values may be sent and summed in bfloat16 or wider, within the bound.
A program may use at most 64 MiB of HBM per device.

v0:
```python
import functools
import math

import jax
import jax.numpy as jnp
from jax import lax
from jax.experimental import pallas as pl
from jax.experimental.pallas import tpu as pltpu
from jax.sharding import PartitionSpec as P

SPACING = 512
NS_ITERS = 6
LANES = 128
META = 16
BASE = 64
F32 = jnp.float32
BF16 = jnp.bfloat16
NT = (((1,), (1,)), ((), ()))


def halves(x):
    hi = x.astype(BF16)
    return hi, (x - hi.astype(F32)).astype(BF16)


def stationary(hi, lo):
    row = jnp.concatenate([hi, lo], axis=1)
    return jnp.concatenate([row, row], axis=0)


def times(left, weights):
    width = weights.shape[1] // 2
    hi, lo = halves(left)
    out = jnp.dot(jnp.concatenate([hi, lo], axis=1), weights, preferred_element_type=F32)
    return out[:, :width] + out[:, width:]


def weights_kernel(
    tiles, lags, slots, group, columns,
    pert_hbm, innov_hbm, rinv_hbm, tile_hbm, col_hbm, count_hbm, ens_hbm,
    out_hbm,
    ens, out, move_sem,
    innov_ref, rinv_ref, tile_ref, col_ref, count_ref, load_sem,
    msg, snd, rcv, acc, to_left, to_right, from_left, from_right, mine, theirs,
    a2a_send, a2a_recv, halo_send, halo_recv, lag_send, lag_recv,
):
    members, own = pert_hbm.shape
    points = columns // SPACING
    half = points // 2
    radius = columns // 2
    pair = 2 * members
    sent = members + META // 2
    me = lax.axis_index("space")
    my_lag = lax.axis_index("lag")

    barrier = pltpu.get_barrier_semaphore()
    order = range(tiles - 1, 0, -1)
    for step in order:
        pl.semaphore_signal(barrier, inc=1, device_id={"space": lax.rem(me + step, tiles)})
    for step in range(1, lags):
        pl.semaphore_signal(barrier, inc=1, device_id={"lag": lax.rem(my_lag + step, lags)})

    loads = [
        pltpu.make_async_copy(source, dest, load_sem.at[n])
        for n, (source, dest) in enumerate((
            (tile_hbm, tile_ref),
            (count_hbm, count_ref),
            (rinv_hbm, rinv_ref),
            (innov_hbm, innov_ref),
            (col_hbm, col_ref),
            (pert_hbm, msg.at[0:members]),
        ))
    ]
    for load in loads:
        load.start()
    for load in loads:
        load.wait()

    slot_id = lax.broadcasted_iota(jnp.int32, (1, own), 1)
    weight = jnp.where(slot_id < count_ref[0, 0], rinv_ref[...].astype(F32), 0.0)
    column = col_ref[...]
    col_hi = (column // BASE).astype(F32)
    col_lo = (column % BASE).astype(F32)
    row = lax.broadcasted_iota(jnp.int32, (META, own), 0)
    meta = jnp.where(row == 0, weight, 0.0)
    meta = jnp.where(row == 1, innov_ref[...].astype(F32), meta)
    meta = jnp.where(row == 2, col_hi, meta)
    meta = jnp.where(row == 3, col_lo, meta)
    msg[members:, :] = meta.astype(BF16)

    target = tile_ref[...]
    hits = jnp.where(target == lax.broadcasted_iota(jnp.int32, (tiles, own), 0), 1.0, 0.0)
    tri = jnp.where(
        lax.broadcasted_iota(jnp.int32, (LANES, LANES), 0)
        < lax.broadcasted_iota(jnp.int32, (LANES, LANES), 1),
        1.0, 0.0,
    ).astype(BF16)
    seen = jnp.zeros((tiles, 1), F32)
    ranks = []
    for b in range(own // LANES):
        block = hits[:, b * LANES : (b + 1) * LANES]
        ahead = jnp.dot(block.astype(BF16), tri, preferred_element_type=F32) + seen
        ranks.append(jnp.sum(ahead * block, axis=0, keepdims=True))
        seen = seen + jnp.sum(block, axis=1, keepdims=True)
    rank = jnp.concatenate(ranks, axis=1).astype(jnp.int32)
    key = target * slots + rank
    place = lax.broadcasted_iota(jnp.int32, (slots, own), 0)
    message = msg[...]

    def bucket(dest):
        chosen = jnp.where(place == key - dest * slots, 1.0, 0.0).astype(BF16)
        return lax.dot_general(message, chosen, NT, preferred_element_type=F32).astype(BF16)

    def a2a(step):
        return pltpu.make_async_remote_copy(
            src_ref=snd.at[step, 0:sent], dst_ref=rcv.at[step, 0:sent],
            send_sem=a2a_send.at[step], recv_sem=a2a_recv.at[step],
            device_id={"space": lax.rem(me + step, tiles)},
        )

    for step in order:
        snd[step] = bucket(lax.rem(me + step, tiles))
    rcv[0] = bucket(me)
    for step in order:
        rcv[step, sent:] = jnp.zeros((members + META - sent, slots), BF16)
    pl.semaphore_wait(barrier, tiles - 1 + lags - 1)
    for step in order:
        a2a(step).start()

    ens_load = pltpu.make_async_copy(ens_hbm, ens, move_sem.at[0])
    ens_load.start()
    arrivals = [0] + list(order)
    for first in range(0, tiles, group):
        for step in arrivals[max(first, 1) : first + group]:
            a2a(step).wait_recv()
        obs = jnp.concatenate([rcv[step] for step in arrivals[first : first + group]], axis=1)
        pert = obs[0:members].astype(F32)
        info = obs[members:].astype(F32)
        obs_weight = info[0:1]
        places = info[2:3] * BASE + info[3:4]

        def moments(ks, obs=obs, pert=pert, places=places, obs_weight=obs_weight, first=first):
            for k in ks:
                center = float((k - half) * SPACING + SPACING // 2)
                taper = jnp.maximum(1.0 - jnp.abs(places - center) / radius, 0.0)
                rho = taper * taper * obs_weight
                scaled = (pert * rho).astype(BF16)
                part = lax.dot_general(scaled, obs, NT, preferred_element_type=F32)
                if first == 0:
                    acc[k] = part
                else:
                    acc[k] += part

        if first + group < tiles:
            moments(range(points + 2 * half))

    lane = lax.broadcasted_iota(jnp.int32, (members, pair), 1)
    low = lane < members

    def joined(a, b):
        return jnp.concatenate([acc[a, :, 0:members], acc[b, :, 0:members]], axis=1)

    def drive_of(a):
        return acc[a, :, members + 1 : members + 2]

    left_copy = pltpu.make_async_remote_copy(
        src_ref=to_left, dst_ref=from_right, send_sem=halo_send.at[0], recv_sem=halo_recv.at[0],
        device_id={"space": lax.rem(me + tiles - 1, tiles)},
    )
    right_copy = pltpu.make_async_remote_copy(
        src_ref=to_right, dst_ref=from_left, send_sem=halo_send.at[1], recv_sem=halo_recv.at[1],
        device_id={"space": lax.rem(me + 1, tiles)},
    )

    pairs_side = (half + 2) // 2
    last = points + 2 * half - 1
    moments(range(half + 1))
    left_own = jnp.concatenate([jnp.zeros((members, members), F32), acc[0, :, 0:members]], axis=1)
    for j in range(half + 1):
        left_own = jnp.where(lane == j, drive_of(j), left_own)
    to_left[0] = left_own
    for i in range(1, pairs_side):
        to_left[i] = joined(2 * i - 1, 2 * i)
    moments(range(last - half, last + 1))
    left_copy.start()
    right_own = jnp.concatenate([acc[last, :, 0:members], jnp.zeros((members, members), F32)], axis=1)
    for j in range(half + 1):
        right_own = jnp.where(lane == members + j, drive_of(last - half + j), right_own)
    to_right[pairs_side - 1] = right_own
    for i in range(pairs_side - 1):
        to_right[i] = joined(last - half + 2 * i, last - half + 2 * i + 1)

    moments(range(half + 1, half + 3))
    right_copy.start()
    moments(range(half + 3, last - half))

    eye = jnp.where(
        lax.rem(lane, members) == lax.broadcasted_iota(jnp.int32, (members, pair), 0), 1.0, 0.0
    )
    mask_low = jnp.where(low, 1.0, 0.0).astype(BF16)
    mask_high = jnp.where(low, 0.0, 1.0).astype(BF16)

    def diagonal(x):
        return jnp.concatenate([x * mask_low, x * mask_high], axis=0)

    def blocks(x):
        hi, lo = halves(x)
        return stationary(diagonal(hi), diagonal(lo))


    count = (points + 2) // 2
    own_pairs = [joined(half - 1 + 2 * i, half + 2 * i) for i in range(count)]
    own_drives = [drive_of(half - 1 + j) for j in range(points + 2)]
    left_copy.wait_recv()
    right_copy.wait_recv()
    lefts = [from_left[i] for i in range(pairs_side)]
    rights = [from_right[i] for i in range(pairs_side)]

    grams, drives = [], []
    for i in range(count):
        total = own_pairs[i] + (members - 1.0) * eye
        if i < pairs_side - 1:
            total = total + lefts[i]
        elif i == pairs_side - 1:
            total = total + jnp.where(low, lefts[i], rights[0])
        else:
            total = total + rights[i - pairs_side + 1]
        grams.append(total)
    for j in range(points + 2):
        if j <= half:
            other = lefts[pairs_side - 1][:, members + j : members + j + 1]
        else:
            other = rights[0][:, j - half - 1 : j - half]
        drives.append(own_drives[j] + other)

    uppers, lowers, scales = [], [], []
    for total in grams:
        squares = jnp.sum(total * total, axis=0, keepdims=True)
        row_low = lax.broadcasted_iota(jnp.int32, (1, pair), 1) < members
        sum_low = jnp.sum(jnp.where(row_low, squares, 0.0), axis=1, keepdims=True)
        sum_high = jnp.sum(jnp.where(row_low, 0.0, squares), axis=1, keepdims=True)
        scale = jnp.sqrt(jnp.where(row_low, sum_low, sum_high))
        scales.append(scale)
        uppers.append(total / scale)

    for sweep in range(NS_ITERS):
        if sweep == 0:
            middles = [1.5 * eye - 0.5 * up for up in uppers]
            lowers = middles
            uppers = [times(up, blocks(mid)) for up, mid in zip(uppers, middles)]
        else:
            middles = [
                1.5 * eye - 0.5 * times(lo, blocks(up)) for lo, up in zip(lowers, uppers)
            ]
            if sweep < NS_ITERS - 1:
                both = [
                    times(jnp.concatenate([up, lo], axis=0), blocks(mid))
                    for up, lo, mid in zip(uppers, lowers, middles)
                ]
                uppers = [x[0:members] for x in both]
                lowers = [x[members:] for x in both]
            else:
                lowers = [times(lo, blocks(mid)) for lo, mid in zip(lowers, middles)]

    results = []
    for i in range(count):
        root = lowers[i] / jnp.sqrt(scales[i])
        top = jnp.where(low, drives[2 * i], 0.0)
        bottom = jnp.where(low, 0.0, drives[2 * i + 1])
        hi, lo = halves(jnp.concatenate([top, bottom], axis=0))
        inner = times(root, stationary(hi, lo))
        shift = times(root, blocks(inner))
        full = math.sqrt(members - 1.0) * root + shift
        results.append(full - jnp.mean(full, axis=0, keepdims=True) + 1.0 / members)
    for i in range(count):
        mine[i] = results[i]

    def lag_copy(step):
        return pltpu.make_async_remote_copy(
            src_ref=mine, dst_ref=theirs.at[step - 1],
            send_sem=lag_send.at[step - 1], recv_sem=lag_recv.at[step - 1],
            device_id={"lag": lax.rem(my_lag + lags - step, lags)},
        )

    for step in range(1, lags):
        lag_copy(step).start()
    for step in range(1, lags):
        lag_copy(step).wait_recv()
        later = my_lag + step < lags
        for i in range(count):
            longer = times(results[i], blocks(theirs[step - 1, i]))
            results[i] = jnp.where(later, longer, results[i])
    turned = jnp.concatenate([results[i].T.astype(BF16) for i in range(count)], axis=0)
    ens_load.wait()
    stores = []
    half_span = SPACING // 2
    for s in range(points + 1):
        start = max(s * SPACING - half_span, 0)
        stop = min(s * SPACING + half_span, columns)
        both = jnp.dot(
            turned[s * members : (s + 2) * members], ens[:, start:stop],
            preferred_element_type=F32,
        )
        along = lax.broadcasted_iota(jnp.int32, (1, stop - start), 1).astype(F32)
        second = (along + float(start - (s * SPACING - half_span))) / SPACING
        mixed = both[0:members] * (1.0 - second) + both[members:] * second
        out[:, start:stop] = mixed.astype(BF16)
        if s % 3 == 2:
            first = max((s - 2) * SPACING - half_span, 0)
            store = pltpu.make_async_copy(
                out.at[:, first:stop], out_hbm.at[:, first:stop], move_sem.at[1 + s // 3]
            )
            store.start()
            stores.append(store)
    for store in stores:
        store.wait()

    for step in range(1, tiles):
        a2a(step).wait_send()
    left_copy.wait_send()
    right_copy.wait_send()
    for step in range(1, lags):
        lag_copy(step).wait_send()


def per_device(ensemble, obs_pert, obs_innov, obs_rinv, obs_tile, obs_column, obs_count):
    members, columns = ensemble.shape[1:]
    own = obs_pert.shape[2]
    tiles, lags = lax.axis_size("space"), lax.axis_size("lag")
    slot_size = max(2, 2 * own // tiles)
    slots = -(-slot_size // LANES) * LANES
    group = 4
    points = columns // SPACING
    half = points // 2
    count = (points + 2) // 2
    pair = 2 * members
    rows = members + META
    side = ((half + 2) // 2, members, pair)
    products = pl.pallas_call(
        functools.partial(weights_kernel, tiles, lags, slots, group, columns),
        out_shape=jax.ShapeDtypeStruct((members, columns), BF16),
        in_specs=[pl.BlockSpec(memory_space=pltpu.HBM)] * 7,
        out_specs=pl.BlockSpec(memory_space=pltpu.HBM),
        scratch_shapes=[
            pltpu.VMEM((members, columns), BF16),
            pltpu.VMEM((members, columns), BF16),
            pltpu.SemaphoreType.DMA((1 + (points + 1) // 3,)),
            pltpu.VMEM((1, own), BF16),
            pltpu.VMEM((1, own), BF16),
            pltpu.VMEM((1, own), jnp.int32),
            pltpu.VMEM((1, own), jnp.int32),
            pltpu.SMEM((1, 1), jnp.int32),
            pltpu.SemaphoreType.DMA((6,)),
            pltpu.VMEM((rows, own), BF16),
            pltpu.VMEM((tiles, rows, slots), BF16),
            pltpu.VMEM((tiles, rows, slots), BF16),
            pltpu.VMEM((points + 2 * half, members, rows), F32),
            pltpu.VMEM(side, F32),
            pltpu.VMEM(side, F32),
            pltpu.VMEM(side, F32),
            pltpu.VMEM(side, F32),
            pltpu.VMEM((count, members, pair), F32),
            pltpu.VMEM((max(lags - 1, 1), count, members, pair), F32),
            pltpu.SemaphoreType.DMA((tiles,)),
            pltpu.SemaphoreType.DMA((tiles,)),
            pltpu.SemaphoreType.DMA((2,)),
            pltpu.SemaphoreType.DMA((2,)),
            pltpu.SemaphoreType.DMA((max(lags - 1, 1),)),
            pltpu.SemaphoreType.DMA((max(lags - 1, 1),)),
        ],
        compiler_params=pltpu.CompilerParams(collective_id=0, has_side_effects=True),
        name="ensemble_weights",
    )(obs_pert[0], obs_innov, obs_rinv, obs_tile[:, :, 0], obs_column, obs_count, ensemble[0])
    return products[None]


def solution(mesh):
    return jax.shard_map(
        per_device,
        mesh=mesh,
        in_specs=(
            P("lag", None, "space"),
            P("lag", None, "space"),
            P("lag", "space"),
            P("lag", "space"),
            P("lag", "space", None),
            P("lag", "space"),
            P("lag", "space"),
        ),
        out_specs=P("lag", None, "space"),
        check_vma=False,
    )
```

profile of v0, /device:TPU:1, one launch (start us, length us, event | category | flops | bytes accessed | tf_op | source)
XLA Modules:
  0.0 28.3 jit_solution(9435876501087664637)
XLA Ops:
  0.7 25.8 %ensemble_weights.1 = bf16[64,4096]{1,0:T(8,128)(2,1)} custom-call(bf16[64,1024]{1,0:T(8,128)(2,1)} %bitcast.6, bf16[1,1024]{1,0:T(2,128)(2,1)} %innov_hbm.1, bf16[1,1024]{1,0:T(2,128)(2,1)} %rinv_hbm.1, s32[1,1024]{1,0:T(1,128)} %bitcast.7, s32[1,1024]{1,0:T(1,128)} %col_hbm.1, s32[1,1]{1,0:T(1,128)S(6)} %copy.9.count_hbm, bf16[64,4096]{1,0:T(8,128)(2,1)} %bitcast.5), custom_call_target="tpu_custom_call" | custom-call | tf_op jit(solution)/shard_map/ensemble_weights/pallas_call | solution.py:339
  26.5 1.9 %copy.10 = bf16[1,64,4096]{2,1,0:T(8,128)(2,1)} copy(bf16[1,64,4096]{2,1,0:T(8,128)(2,1)} %bitcast.4) | data formatting | bytes 1048576
where the time goes:
time: 28.5 us; the launch traced here: 28.3 us
  Pallas kernels  25.8 us (91%)
  local copies, waits for them, and re-layouts  1.87 us (7%)
  between operations  0.66 us (2%)
    pallas_call x1, Pallas kernels, per_device(): pl.pallas_call(functools.partial(weights_kernel, tiles, lags, slots, grou...  25.8 us
    unnamed x1, local copies, waits for them, and re-layouts  1.87 us

commit v1 on v0

--- a/solution.py
+++ b/solution.py
@@ -10,6 +10,9 @@
 
 SPACING = 512
 NS_ITERS = 6
+AHEAD = 3
+EDGE = 6
+LIMIT = 24 * 1024 * 1024
 LANES = 128
 META = 16
 BASE = 64
@@ -35,14 +38,25 @@
     return out[:, :width] + out[:, width:]
 
 
+def partner(me, step, tiles):
+    if tiles & (tiles - 1):
+        return lax.rem(me + step, tiles)
+    other, bit = me, 1
+    while bit < tiles:
+        if step & bit:
+            other = other + bit - 2 * bit * lax.rem(lax.div(me, bit), 2)
+        bit *= 2
+    return other
+
+
 def weights_kernel(
     tiles, lags, slots, group, columns,
     pert_hbm, innov_hbm, rinv_hbm, tile_hbm, col_hbm, count_hbm, ens_hbm,
-    out_hbm,
-    ens, out, move_sem,
+    turned, ens,
+    move_sem,
     innov_ref, rinv_ref, tile_ref, col_ref, count_ref, load_sem,
     msg, snd, rcv, acc, to_left, to_right, from_left, from_right, mine, theirs,
-    a2a_send, a2a_recv, halo_send, halo_recv, lag_send, lag_recv,
+    a2a_send, a2a_recv, halo_send, halo_recv, lag_send, lag_recv, product, edge, edge_rcv, edge_acc, edge_send, edge_recv,
 ):
     members, own = pert_hbm.shape
     points = columns // SPACING
@@ -56,7 +70,7 @@
     barrier = pltpu.get_barrier_semaphore()
     order = range(tiles - 1, 0, -1)
     for step in order:
-        pl.semaphore_signal(barrier, inc=1, device_id={"space": lax.rem(me + step, tiles)})
+        pl.semaphore_signal(barrier, inc=1, device_id={"space": partner(me, step, tiles)})
     for step in range(1, lags):
         pl.semaphore_signal(barrier, inc=1, device_id={"lag": lax.rem(my_lag + step, lags)})
 
@@ -102,54 +116,87 @@
         ahead = jnp.dot(block.astype(BF16), tri, preferred_element_type=F32) + seen
         ranks.append(jnp.sum(ahead * block, axis=0, keepdims=True))
         seen = seen + jnp.sum(block, axis=1, keepdims=True)
-    rank = jnp.concatenate(ranks, axis=1).astype(jnp.int32)
-    key = target * slots + rank
-    place = lax.broadcasted_iota(jnp.int32, (slots, own), 0)
+    rank = jnp.concatenate(ranks, axis=1)
+    place = lax.broadcasted_iota(jnp.int32, (slots, own), 0).astype(F32).astype(BF16)
     message = msg[...]
 
     def bucket(dest):
-        chosen = jnp.where(place == key - dest * slots, 1.0, 0.0).astype(BF16)
+        wanted = jnp.where(target == dest, rank, -1.0).astype(BF16)
+        chosen = jnp.where(place == wanted, jnp.ones((), BF16), jnp.zeros((), BF16))
         return lax.dot_general(message, chosen, NT, preferred_element_type=F32).astype(BF16)
 
     def a2a(step):
         return pltpu.make_async_remote_copy(
             src_ref=snd.at[step, 0:sent], dst_ref=rcv.at[step, 0:sent],
             send_sem=a2a_send.at[step], recv_sem=a2a_recv.at[step],
-            device_id={"space": lax.rem(me + step, tiles)},
+            device_id={"space": partner(me, step, tiles)},
         )
 
-    for step in order:
-        snd[step] = bucket(lax.rem(me + step, tiles))
+    def edge_copy(source):
+        return pltpu.make_async_remote_copy(
+            src_ref=edge.at[0:sent], dst_ref=edge_rcv.at[source, 0:sent],
+            send_sem=edge_send.at[0], recv_sem=edge_recv.at[source],
+            device_id={"space": 0 * me},
+        )
+
+    edge[...] = bucket(tiles - 1)
+    for step in order[:AHEAD]:
+        snd[step] = bucket(partner(me, step, tiles))
+    pl.semaphore_wait(barrier, tiles - 1 + lags - 1)
+    for n, step in enumerate(order):
+        if n >= AHEAD:
+            snd[step] = bucket(partner(me, step, tiles))
+        if n == EDGE:
+            @pl.when(me > 0)
+            def _():
+                edge_copy(me).start()
+        if n >= AHEAD - 1:
+            for early in order[0 if n == AHEAD - 1 else n - 1 : n] if n >= AHEAD else order[: AHEAD - 1]:
+                a2a(early).start()
+    a2a(order[-1]).start()
     rcv[0] = bucket(me)
     for step in order:
         rcv[step, sent:] = jnp.zeros((members + META - sent, slots), BF16)
-    pl.semaphore_wait(barrier, tiles - 1 + lags - 1)
-    for step in order:
-        a2a(step).start()
 
     ens_load = pltpu.make_async_copy(ens_hbm, ens, move_sem.at[0])
     ens_load.start()
-    arrivals = [0] + list(order)
+    arrivals = list(range(tiles))
+
+    def partials(obs, ks, into, base, fresh):
+        pert = obs[0:members].astype(F32)
+        info = obs[members:].astype(F32)
+        obs_weight = info[0:1]
+        places = info[2:3] * BASE + info[3:4]
+        for k in ks:
+            center = float((k - half) * SPACING + SPACING // 2)
+            taper = jnp.maximum(1.0 - jnp.abs(places - center) / radius, 0.0)
+            rho = taper * taper * obs_weight
+            scaled = (pert * rho).astype(BF16)
+            part = lax.dot_general(scaled, obs, NT, preferred_element_type=F32)
+            if fresh:
+                into[k - base] = part
+            else:
+                into[k - base] += part
+
     for first in range(0, tiles, group):
         for step in arrivals[max(first, 1) : first + group]:
             a2a(step).wait_recv()
         obs = jnp.concatenate([rcv[step] for step in arrivals[first : first + group]], axis=1)
-        pert = obs[0:members].astype(F32)
-        info = obs[members:].astype(F32)
-        obs_weight = info[0:1]
-        places = info[2:3] * BASE + info[3:4]
-
-        def moments(ks, obs=obs, pert=pert, places=places, obs_weight=obs_weight, first=first):
-            for k in ks:
-                center = float((k - half) * SPACING + SPACING // 2)
-                taper = jnp.maximum(1.0 - jnp.abs(places - center) / radius, 0.0)
-                rho = taper * taper * obs_weight
-                scaled = (pert * rho).astype(BF16)
-                part = lax.dot_general(scaled, obs, NT, preferred_element_type=F32)
-                if first == 0:
-                    acc[k] = part
-                else:
-                    acc[k] += part
+
+        def moments(ks, obs=obs, first=first):
+            partials(obs, ks, acc, 0, first == 0)
+
+        @pl.when(me == 0)
+        def _(first=first):
+            for step in arrivals[max(first, 1) : first + group]:
+                edge_copy(step).wait_recv()
+            near = [
+                edge_rcv[step] if step else edge[...] for step in arrivals[first : first + group]
+            ]
+            partials(
+                jnp.concatenate(near, axis=1), range(points + half - 1, points + 2 * half),
+                edge_acc, points + half - 1, first == 0,
+            )
 
         if first + group < tiles:
             moments(range(points + 2 * half))
@@ -157,11 +204,11 @@
     lane = lax.broadcasted_iota(jnp.int32, (members, pair), 1)
     low = lane < members
 
-    def joined(a, b):
-        return jnp.concatenate([acc[a, :, 0:members], acc[b, :, 0:members]], axis=1)
-
-    def drive_of(a):
-        return acc[a, :, members + 1 : members + 2]
+    def joined(a, b, source=acc):
+        return jnp.concatenate([source[a, :, 0:members], source[b, :, 0:members]], axis=1)
+
+    def drive_of(a, source=acc):
+        return source[a, :, members + 1 : members + 2]
 
     left_copy = pltpu.make_async_remote_copy(
         src_ref=to_left, dst_ref=from_right, send_sem=halo_send.at[0], recv_sem=halo_recv.at[0],
@@ -172,26 +219,67 @@
         device_id={"space": lax.rem(me + 1, tiles)},
     )
 
-    pairs_side = (half + 2) // 2
+    fold = members // 2
+    row = lax.broadcasted_iota(jnp.int32, (members, pair), 0)
+    within = lax.rem(lane, members)
+    strip = lax.broadcasted_iota(jnp.int32, (fold, pair), 1) - members
+
+    def packed(single, ks, source=acc):
+        first = [joined(ks[n], ks[n + 1], source) for n in range(0, half, 2)]
+        columns = [drive_of(k, source) for k in sorted([single, *ks])]
+        for other in first[1::2]:
+            diag = jnp.where(row == within, other, 0.0)
+            columns.append(jnp.sum(jnp.where(low, diag, 0.0), axis=1, keepdims=True))
+            columns.append(jnp.sum(jnp.where(low, 0.0, diag), axis=1, keepdims=True))
+        parts = [
+            jnp.where(row <= within, first[n], first[n + 1]) for n in range(0, half // 2, 2)
+        ]
+        tail = jnp.concatenate(
+            [source[single, 0:fold, 0:members], source[single, fold:members, 0:members]], axis=1
+        )
+        for n, column in enumerate(columns):
+            tail = jnp.where(strip == 2 * n, column[0:fold], tail)
+            tail = jnp.where(strip == 2 * n + 1, column[fold:], tail)
+        return jnp.concatenate([*parts, tail], axis=0)
+
+    def unpacked(ref):
+        tail = ref[members * (half // 4) :]
+
+        def column(n):
+            return jnp.concatenate(
+                [
+                    tail[:, members + 2 * n : members + 2 * n + 1],
+                    tail[:, members + 2 * n + 1 : members + 2 * n + 2],
+                ],
+                axis=0,
+            )
+
+        pairs = []
+        for n in range(half // 4):
+            part = ref[n * members : (n + 1) * members]
+            turned_part = jnp.concatenate([part[:, 0:members].T, part[:, members:].T], axis=1)
+            pairs.append(jnp.where(row <= within, part, turned_part))
+            diag = jnp.where(low, column(half + 1 + 2 * n), column(half + 2 + 2 * n))
+            other = jnp.where(row == within, diag, turned_part)
+            pairs.append(jnp.where(row > within, part, other))
+        corner = tail[:, 0:members].T[fold:]
+        bottom = jnp.concatenate([corner, tail[:, members + fold :]], axis=1)
+        single = jnp.concatenate([tail[:, 0:members], bottom], axis=0)
+        return pairs, single, [column(n) for n in range(half + 1)]
+
     last = points + 2 * half - 1
     moments(range(half + 1))
-    left_own = jnp.concatenate([jnp.zeros((members, members), F32), acc[0, :, 0:members]], axis=1)
-    for j in range(half + 1):
-        left_own = jnp.where(lane == j, drive_of(j), left_own)
-    to_left[0] = left_own
-    for i in range(1, pairs_side):
-        to_left[i] = joined(2 * i - 1, 2 * i)
+    to_left[...] = packed(0, list(range(1, half + 1)))
     moments(range(last - half, last + 1))
     left_copy.start()
-    right_own = jnp.concatenate([acc[last, :, 0:members], jnp.zeros((members, members), F32)], axis=1)
-    for j in range(half + 1):
-        right_own = jnp.where(lane == members + j, drive_of(last - half + j), right_own)
-    to_right[pairs_side - 1] = right_own
-    for i in range(pairs_side - 1):
-        to_right[i] = joined(last - half + 2 * i, last - half + 2 * i + 1)
+    to_right[...] = packed(last, list(range(last - half, last)))
 
     moments(range(half + 1, half + 3))
-    right_copy.start()
+
+    @pl.when(me < tiles - 1)
+    def _():
+        right_copy.start()
+
     moments(range(half + 3, last - half))
 
     eye = jnp.where(
@@ -212,26 +300,31 @@
     own_pairs = [joined(half - 1 + 2 * i, half + 2 * i) for i in range(count)]
     own_drives = [drive_of(half - 1 + j) for j in range(points + 2)]
     left_copy.wait_recv()
-    right_copy.wait_recv()
-    lefts = [from_left[i] for i in range(pairs_side)]
-    rights = [from_right[i] for i in range(pairs_side)]
-
-    grams, drives = [], []
+
+    @pl.when(me > 0)
+    def _():
+        right_copy.wait_recv()
+
+    @pl.when(me == 0)
+    def _():
+        from_left[...] = packed(half, list(range(half)), edge_acc)
+
+    lefts, left_single, left_drives = unpacked(from_left)
+    rights, right_single, right_drives = unpacked(from_right)
+
+    grams = []
     for i in range(count):
         total = own_pairs[i] + (members - 1.0) * eye
-        if i < pairs_side - 1:
+        if i < half // 2:
             total = total + lefts[i]
-        elif i == pairs_side - 1:
-            total = total + jnp.where(low, lefts[i], rights[0])
+        elif i == half // 2:
+            total = total + jnp.concatenate([left_single, right_single], axis=1)
         else:
-            total = total + rights[i - pairs_side + 1]
+            total = total + rights[i - half // 2 - 1]
         grams.append(total)
-    for j in range(points + 2):
-        if j <= half:
-            other = lefts[pairs_side - 1][:, members + j : members + j + 1]
-        else:
-            other = rights[0][:, j - half - 1 : j - half]
-        drives.append(own_drives[j] + other)
+    drives = [
+        own + other for own, other in zip(own_drives, [*left_drives, *right_drives])
+    ]
 
     uppers, lowers, scales = [], [], []
     for total in grams:
@@ -274,6 +367,7 @@
         results.append(full - jnp.mean(full, axis=0, keepdims=True) + 1.0 / members)
     for i in range(count):
         mine[i] = results[i]
+        product[i] = results[i]
 
     def lag_copy(step):
         return pltpu.make_async_remote_copy(
@@ -283,15 +377,40 @@
         )
 
     for step in range(1, lags):
-        lag_copy(step).start()
+        @pl.when(my_lag >= step)
+        def _(step=step):
+            lag_copy(step).start()
     for step in range(1, lags):
-        lag_copy(step).wait_recv()
-        later = my_lag + step < lags
-        for i in range(count):
-            longer = times(results[i], blocks(theirs[step - 1, i]))
-            results[i] = jnp.where(later, longer, results[i])
-    turned = jnp.concatenate([results[i].T.astype(BF16) for i in range(count)], axis=0)
+        @pl.when(my_lag + step < lags)
+        def _(step=step):
+            lag_copy(step).wait_recv()
+            for i in range(count):
+                product[i] = times(product[i], blocks(theirs[step - 1, i]))
+    for i in range(count):
+        turned[i * pair : (i + 1) * pair] = product[i].T.astype(BF16)
     ens_load.wait()
+
+    for step in range(1, tiles):
+        a2a(step).wait_send()
+    left_copy.wait_send()
+
+    @pl.when(me < tiles - 1)
+    def _():
+        right_copy.wait_send()
+
+    @pl.when(me > 0)
+    def _():
+        edge_copy(me).wait_send()
+
+    for step in range(1, lags):
+        @pl.when(my_lag >= step)
+        def _(step=step):
+            lag_copy(step).wait_send()
+
+
+def apply_kernel(turned, ens, out_hbm, out, store_sem):
+    members, columns = ens.shape
+    points = columns // SPACING
     stores = []
     half_span = SPACING // 2
     for s in range(points + 1):
@@ -308,19 +427,12 @@
         if s % 3 == 2:
             first = max((s - 2) * SPACING - half_span, 0)
             store = pltpu.make_async_copy(
-                out.at[:, first:stop], out_hbm.at[:, first:stop], move_sem.at[1 + s // 3]
+                out.at[:, first:stop], out_hbm.at[:, first:stop], store_sem.at[s // 3]
             )
             store.start()
             stores.append(store)
     for store in stores:
         store.wait()
-
-    for step in range(1, tiles):
-        a2a(step).wait_send()
-    left_copy.wait_send()
-    right_copy.wait_send()
-    for step in range(1, lags):
-        lag_copy(step).wait_send()
 
 
 def per_device(ensemble, obs_pert, obs_innov, obs_rinv, obs_tile, obs_column, obs_count):
@@ -335,16 +447,14 @@
     count = (points + 2) // 2
     pair = 2 * members
     rows = members + META
-    side = ((half + 2) // 2, members, pair)
-    products = pl.pallas_call(
+    side = (members * (half // 4) + members // 2, pair)
+    turned, held = pl.pallas_call(
         functools.partial(weights_kernel, tiles, lags, slots, group, columns),
-        out_shape=jax.ShapeDtypeStruct((members, columns), BF16),
+        out_shape=(pltpu.VMEM((count * pair, members), BF16), pltpu.VMEM((members, columns), BF16)),
         in_specs=[pl.BlockSpec(memory_space=pltpu.HBM)] * 7,
-        out_specs=pl.BlockSpec(memory_space=pltpu.HBM),
+        out_specs=[pl.BlockSpec(memory_space=pltpu.VMEM)] * 2,
         scratch_shapes=[
-            pltpu.VMEM((members, columns), BF16),
-            pltpu.VMEM((members, columns), BF16),
-            pltpu.SemaphoreType.DMA((1 + (points + 1) // 3,)),
+            pltpu.SemaphoreType.DMA((1,)),
             pltpu.VMEM((1, own), BF16),
             pltpu.VMEM((1, own), BF16),
             pltpu.VMEM((1, own), jnp.int32),
@@ -367,11 +477,36 @@
             pltpu.SemaphoreType.DMA((2,)),
             pltpu.SemaphoreType.DMA((max(lags - 1, 1),)),
             pltpu.SemaphoreType.DMA((max(lags - 1, 1),)),
+            pltpu.VMEM((count, members, pair), F32),
+            pltpu.VMEM((rows, slots), BF16),
+            pltpu.VMEM((tiles, rows, slots), BF16),
+            pltpu.VMEM((half + 1, members, rows), F32),
+            pltpu.SemaphoreType.DMA((1,)),
+            pltpu.SemaphoreType.DMA((tiles,)),
         ],
-        compiler_params=pltpu.CompilerParams(collective_id=0, has_side_effects=True),
+        compiler_params=pltpu.CompilerParams(
+            collective_id=0, has_side_effects=True, vmem_limit_bytes=LIMIT
+        ),
         name="ensemble_weights",
-    )(obs_pert[0], obs_innov, obs_rinv, obs_tile[:, :, 0], obs_column, obs_count, ensemble[0])
-    return products[None]
+    )(*(
+        x if x.size == 1 else pltpu.with_memory_space_constraint(x, pltpu.HBM)
+        for x in (
+            obs_pert[0], obs_innov, obs_rinv, obs_tile[:, :, 0], obs_column, obs_count, ensemble[0]
+        )
+    ))
+    analysis = pl.pallas_call(
+        apply_kernel,
+        out_shape=jax.ShapeDtypeStruct((members, columns), BF16),
+        in_specs=[pl.BlockSpec(memory_space=pltpu.VMEM)] * 2,
+        out_specs=pl.BlockSpec(memory_space=pltpu.HBM),
+        scratch_shapes=[
+            pltpu.VMEM((members, columns), BF16),
+            pltpu.SemaphoreType.DMA(((points + 1) // 3,)),
+        ],
+        compiler_params=pltpu.CompilerParams(vmem_limit_bytes=LIMIT),
+        name="apply_weights",
+    )(turned, held)
+    return analysis[None]
 
 
 def solution(mesh):

time: 28.5 us -> 25.9 us (0.909)
  the two profiles are of different devices: /device:TPU:1 before, /device:TPU:0 now
where the time goes in v1:
time: 25.9 us; the launch traced here: 25.8 us
  Pallas kernels  25.1 us (97%)
  between operations  0.66 us (3%)
    pallas_call x1, Pallas kernels, per_device(): pl.pallas_call(functools.partial(weights_kernel, tiles, lags, slots, grou...  24 us
    pallas_call x1, Pallas kernels, per_device(): pl.pallas_call(apply_kernel, out_shape=jax.ShapeDtypeStruct((members, col...  1.12 us

profile of v1, /device:TPU:0, one launch (start us, length us, event | category | flops | bytes accessed | tf_op | source)
XLA Modules:
  0.0 25.8 jit_solution(715829009736358122)
XLA Ops:
  0.7 24.0 %ensemble_weights.1 = (bf16[640,64]{1,0:T(8,128)(2,1)S(1)}, bf16[64,4096]{1,0:T(8,128)(2,1)S(1)}) custom-call(bf16[64,1024]{1,0:T(8,128)(2,1)} %bitcast.5, bf16[1,1024]{1,0:T(2,128)(2,1)} %innov_hbm.1, bf16[1,1024]{1,0:T(2,128)(2,1)} %rinv_hbm.1, s32[1,1024]{1,0:T(1,128)} %bitcast.6, s32[1,1024]{1,0:T(1,128)} %col_hbm.1, s32[1,1]{1,0:T(1,128)S(6)} %copy.8.count_hbm, ...), custom_call_target="tpu_custom_call" | custom-call | tf_op jit(solution)/shard_map/ensemble_weights/pallas_call | solution.py:451
  24.6 1.1 %apply_weights.1 = bf16[64,4096]{1,0:T(8,128)(2,1)} custom-call(bf16[640,64]{1,0:T(8,128)(2,1)S(1)} %get-tuple-element.7.turned, bf16[64,4096]{1,0:T(8,128)(2,1)S(1)} %get-tuple-element.8.ens), custom_call_target="tpu_custom_call" | custom-call | tf_op jit(solution)/shard_map/apply_weights/pallas_call | solution.py:497

commit v2 on v1

--- a/solution.py
+++ b/solution.py
@@ -10,8 +10,8 @@
 
 SPACING = 512
 NS_ITERS = 6
-AHEAD = 3
-EDGE = 6
+BATCHES = [2, 2]
+BLOCKS = 4
 LIMIT = 24 * 1024 * 1024
 LANES = 128
 META = 16
@@ -40,7 +40,7 @@
 
 def partner(me, step, tiles):
     if tiles & (tiles - 1):
-        return lax.rem(me + step, tiles)
+        return lax.rem(me + tiles - step, tiles)
     other, bit = me, 1
     while bit < tiles:
         if step & bit:
@@ -56,7 +56,7 @@
     move_sem,
     innov_ref, rinv_ref, tile_ref, col_ref, count_ref, load_sem,
     msg, snd, rcv, acc, to_left, to_right, from_left, from_right, mine, theirs,
-    a2a_send, a2a_recv, halo_send, halo_recv, lag_send, lag_recv, product, edge, edge_rcv, edge_acc, edge_send, edge_recv,
+    a2a_send, a2a_recv, halo_send, halo_recv, lag_send, lag_recv, product, edge, edge_rcv, edge_acc, edge_send, edge_recv, ready,
 ):
     members, own = pert_hbm.shape
     points = columns // SPACING
@@ -68,9 +68,29 @@
     my_lag = lax.axis_index("lag")
 
     barrier = pltpu.get_barrier_semaphore()
-    order = range(tiles - 1, 0, -1)
-    for step in order:
-        pl.semaphore_signal(barrier, inc=1, device_id={"space": partner(me, step, tiles)})
+    blocks_of = BLOCKS if tiles % BLOCKS == 0 else 1
+    wide = tiles // blocks_of
+    mine_block, inner = lax.div(me, wide), lax.rem(me, wide)
+
+    def rank_of(tile):
+        block, place = lax.div(tile, wide), lax.rem(tile, wide)
+        digits, bit = block, 1
+        while bit < wide:
+            digits = digits + lax.rem(lax.div(place, bit), 2)
+            bit *= 2
+        return digits * tiles + tile
+
+    def before(a, b):
+        return lax.div(b - a + span - 1, span)
+
+    span = tiles * (tiles + blocks_of)
+    my_rank = rank_of(me)
+    ranks_of = [rank_of(jnp.int32(tile)) for tile in range(tiles)]
+    earlier = sum(before(r, my_rank) for r in ranks_of)
+    for peer in range(tiles - 1, -1, -1):
+        @pl.when(my_rank < ranks_of[peer])
+        def _(peer=peer):
+            pl.semaphore_signal(barrier, inc=1, device_id={"space": peer})
     for step in range(1, lags):
         pl.semaphore_signal(barrier, inc=1, device_id={"lag": lax.rem(my_lag + step, lags)})
 
@@ -125,12 +145,18 @@
         chosen = jnp.where(place == wanted, jnp.ones((), BF16), jnp.zeros((), BF16))
         return lax.dot_general(message, chosen, NT, preferred_element_type=F32).astype(BF16)
 
-    def a2a(step):
+    def a2a(step, peer=None):
         return pltpu.make_async_remote_copy(
             src_ref=snd.at[step, 0:sent], dst_ref=rcv.at[step, 0:sent],
             send_sem=a2a_send.at[step], recv_sem=a2a_recv.at[step],
-            device_id={"space": partner(me, step, tiles)},
-        )
+            device_id={"space": me if peer is None else peer},
+        )
+
+    pl.semaphore_wait(barrier, earlier + lags - 1)
+    for peer in range(tiles):
+        @pl.when(ranks_of[peer] < my_rank)
+        def _(peer=peer):
+            pl.semaphore_signal(ready.at[me], inc=1, device_id={"space": peer})
 
     def edge_copy(source):
         return pltpu.make_async_remote_copy(
@@ -139,23 +165,35 @@
             device_id={"space": 0 * me},
         )
 
-    edge[...] = bucket(tiles - 1)
-    for step in order[:AHEAD]:
-        snd[step] = bucket(partner(me, step, tiles))
-    pl.semaphore_wait(barrier, tiles - 1 + lags - 1)
-    for n, step in enumerate(order):
-        if n >= AHEAD:
-            snd[step] = bucket(partner(me, step, tiles))
-        if n == EDGE:
+    def step_of(peer):
+        block, place = peer // wide, peer % wide
+        ahead = lax.rem(mine_block + blocks_of - block, blocks_of)
+        return ahead * wide + partner(inner, place, wide)
+
+    def send(peer):
+        @pl.when(my_rank < ranks_of[peer])
+        def _():
+            pl.semaphore_wait(ready.at[peer], 1)
+
+        @pl.when(me != peer)
+        def _():
+            a2a(step_of(peer), jnp.int32(peer)).start()
+
+    done = 0
+    for size in BATCHES + [4] * tiles:
+        batch = range(done, min(done + size, tiles))
+        for peer in batch:
+            snd[step_of(peer)] = bucket(peer)
+        if done == 0:
+            edge[...] = bucket(tiles - 1)
+        for peer in batch:
+            send(peer)
+        if done == 0:
             @pl.when(me > 0)
             def _():
                 edge_copy(me).start()
-        if n >= AHEAD - 1:
-            for early in order[0 if n == AHEAD - 1 else n - 1 : n] if n >= AHEAD else order[: AHEAD - 1]:
-                a2a(early).start()
-    a2a(order[-1]).start()
-    rcv[0] = bucket(me)
-    for step in order:
+        done += size
+    for step in range(1, tiles):
         rcv[step, sent:] = jnp.zeros((members + META - sent, slots), BF16)
 
     ens_load = pltpu.make_async_copy(ens_hbm, ens, move_sem.at[0])
@@ -181,7 +219,9 @@
     for first in range(0, tiles, group):
         for step in arrivals[max(first, 1) : first + group]:
             a2a(step).wait_recv()
-        obs = jnp.concatenate([rcv[step] for step in arrivals[first : first + group]], axis=1)
+        obs = jnp.concatenate(
+            [rcv[step] if step else snd[0] for step in arrivals[first : first + group]], axis=1
+        )
 
         def moments(ks, obs=obs, first=first):
             partials(obs, ks, acc, 0, first == 0)
@@ -483,6 +523,7 @@
             pltpu.VMEM((half + 1, members, rows), F32),
             pltpu.SemaphoreType.DMA((1,)),
             pltpu.SemaphoreType.DMA((tiles,)),
+            pltpu.SemaphoreType.REGULAR((tiles,)),
         ],
         compiler_params=pltpu.CompilerParams(
             collective_id=0, has_side_effects=True, vmem_limit_bytes=LIMIT

time: 25.9 us -> 24 us (0.927)
  Pallas kernels: 25.1 us -> 22.9 us
    pallas_call x1, Pallas kernels: 24 us -> 21.8 us  [per_device(): pl.pallas_call(functools.partial(weights_kernel, tiles, lags, slots, grou...]
where the time goes in v2:
time: 24 us; the launch traced here: 23.6 us
  Pallas kernels  22.9 us (95%)
  between operations  0.66 us (3%)
    pallas_call x1, Pallas kernels, per_device(): pl.pallas_call(functools.partial(weights_kernel, tiles, lags, slots, grou...  21.8 us
    pallas_call x1, Pallas kernels, per_device(): pl.pallas_call(apply_kernel, out_shape=jax.ShapeDtypeStruct((members, col...  1.12 us

profile of v2, /device:TPU:0, one launch (start us, length us, event | category | flops | bytes accessed | tf_op | source)
XLA Modules:
  0.0 23.6 jit_solution(18148711708278882678)
XLA Ops:
  0.7 21.8 %ensemble_weights.1 = (bf16[640,64]{1,0:T(8,128)(2,1)S(1)}, bf16[64,4096]{1,0:T(8,128)(2,1)S(1)}) custom-call(bf16[64,1024]{1,0:T(8,128)(2,1)} %bitcast.5, bf16[1,1024]{1,0:T(2,128)(2,1)} %innov_hbm.1, bf16[1,1024]{1,0:T(2,128)(2,1)} %rinv_hbm.1, s32[1,1024]{1,0:T(1,128)} %bitcast.6, s32[1,1024]{1,0:T(1,128)} %col_hbm.1, s32[1,1]{1,0:T(1,128)S(6)} %copy.8.count_hbm, ...), custom_call_target="tpu_custom_call" | custom-call | tf_op jit(solution)/shard_map/ensemble_weights/pallas_call | solution.py:491
  22.5 1.1 %apply_weights.1 = bf16[64,4096]{1,0:T(8,128)(2,1)} custom-call(bf16[640,64]{1,0:T(8,128)(2,1)S(1)} %get-tuple-element.7.turned, bf16[64,4096]{1,0:T(8,128)(2,1)S(1)} %get-tuple-element.8.ens), custom_call_target="tpu_custom_call" | custom-call | tf_op jit(solution)/shard_map/apply_weights/pallas_call | solution.py:538

commit v3 on v2

--- a/solution.py
+++ b/solution.py
@@ -10,6 +10,7 @@
 
 SPACING = 512
 NS_ITERS = 6
+THIN = 16
 BATCHES = [2, 2]
 BLOCKS = 4
 LIMIT = 24 * 1024 * 1024
@@ -210,7 +211,7 @@
             taper = jnp.maximum(1.0 - jnp.abs(places - center) / radius, 0.0)
             rho = taper * taper * obs_weight
             scaled = (pert * rho).astype(BF16)
-            part = lax.dot_general(scaled, obs, NT, preferred_element_type=F32)
+            part = lax.dot_general(obs, scaled, NT, preferred_element_type=F32)
             if fresh:
                 into[k - base] = part
             else:
@@ -245,10 +246,13 @@
     low = lane < members
 
     def joined(a, b, source=acc):
-        return jnp.concatenate([source[a, :, 0:members], source[b, :, 0:members]], axis=1)
-
-    def drive_of(a, source=acc):
-        return source[a, :, members + 1 : members + 2]
+        return jnp.concatenate([source[a, 0:members], source[b, 0:members]], axis=1)
+
+    def drives_of(a, b, source=acc):
+        none = jnp.zeros((1, members), F32)
+        return jnp.concatenate(
+            [none if k is None else source[k, members + 1 : members + 2] for k in (a, b)], axis=1
+        )
 
     left_copy = pltpu.make_async_remote_copy(
         src_ref=to_left, dst_ref=from_right, send_sem=halo_send.at[0], recv_sem=halo_recv.at[0],
@@ -260,52 +264,44 @@
     )
 
     fold = members // 2
+    extra = members * (half // 4) + fold
     row = lax.broadcasted_iota(jnp.int32, (members, pair), 0)
     within = lax.rem(lane, members)
-    strip = lax.broadcasted_iota(jnp.int32, (fold, pair), 1) - members
 
     def packed(single, ks, source=acc):
         first = [joined(ks[n], ks[n + 1], source) for n in range(0, half, 2)]
-        columns = [drive_of(k, source) for k in sorted([single, *ks])]
-        for other in first[1::2]:
-            diag = jnp.where(row == within, other, 0.0)
-            columns.append(jnp.sum(jnp.where(low, diag, 0.0), axis=1, keepdims=True))
-            columns.append(jnp.sum(jnp.where(low, 0.0, diag), axis=1, keepdims=True))
+        ends = (None, single) if single < ks[0] else (single, None)
+        vectors = [drives_of(ks[n], ks[n + 1], source) for n in range(0, half, 2)]
+        vectors.append(drives_of(*ends, source))
+        vectors += [
+            jnp.sum(jnp.where(row == within, other, 0.0), axis=0, keepdims=True)
+            for other in first[1::2]
+        ]
+        spare = -len(vectors) % 8
+        if spare:
+            vectors.append(jnp.zeros((spare, pair), F32))
         parts = [
             jnp.where(row <= within, first[n], first[n + 1]) for n in range(0, half // 2, 2)
         ]
         tail = jnp.concatenate(
-            [source[single, 0:fold, 0:members], source[single, fold:members, 0:members]], axis=1
-        )
-        for n, column in enumerate(columns):
-            tail = jnp.where(strip == 2 * n, column[0:fold], tail)
-            tail = jnp.where(strip == 2 * n + 1, column[fold:], tail)
-        return jnp.concatenate([*parts, tail], axis=0)
+            [source[single, 0:fold], source[single, fold:members]], axis=1
+        )
+        return jnp.concatenate([*parts, tail, *vectors], axis=0)
 
     def unpacked(ref):
-        tail = ref[members * (half // 4) :]
-
-        def column(n):
-            return jnp.concatenate(
-                [
-                    tail[:, members + 2 * n : members + 2 * n + 1],
-                    tail[:, members + 2 * n + 1 : members + 2 * n + 2],
-                ],
-                axis=0,
-            )
-
         pairs = []
         for n in range(half // 4):
             part = ref[n * members : (n + 1) * members]
-            turned_part = jnp.concatenate([part[:, 0:members].T, part[:, members:].T], axis=1)
-            pairs.append(jnp.where(row <= within, part, turned_part))
-            diag = jnp.where(low, column(half + 1 + 2 * n), column(half + 2 + 2 * n))
-            other = jnp.where(row == within, diag, turned_part)
+            flipped = jnp.concatenate([part[:, 0:members].T, part[:, members:].T], axis=1)
+            pairs.append(jnp.where(row <= within, part, flipped))
+            at = extra + half // 2 + 1 + n
+            other = jnp.where(row == within, ref[at : at + 1], flipped)
             pairs.append(jnp.where(row > within, part, other))
+        tail = ref[extra - fold : extra]
         corner = tail[:, 0:members].T[fold:]
         bottom = jnp.concatenate([corner, tail[:, members + fold :]], axis=1)
         single = jnp.concatenate([tail[:, 0:members], bottom], axis=0)
-        return pairs, single, [column(n) for n in range(half + 1)]
+        return pairs, single, [ref[extra + n : extra + n + 1] for n in range(half // 2 + 1)]
 
     last = points + 2 * half - 1
     moments(range(half + 1))
@@ -338,7 +334,7 @@
 
     count = (points + 2) // 2
     own_pairs = [joined(half - 1 + 2 * i, half + 2 * i) for i in range(count)]
-    own_drives = [drive_of(half - 1 + j) for j in range(points + 2)]
+    own_drives = [drives_of(half - 1 + 2 * i, half + 2 * i) for i in range(count)]
     left_copy.wait_recv()
 
     @pl.when(me > 0)
@@ -363,48 +359,54 @@
             total = total + rights[i - half // 2 - 1]
         grams.append(total)
     drives = [
-        own + other for own, other in zip(own_drives, [*left_drives, *right_drives])
+        own_drives[i]
+        + (left_drives[i] if i < half // 2 else 0.0)
+        + (right_drives[i - half // 2 - 1] if i > half // 2 else 0.0)
+        for i in range(count)
     ]
-
-    uppers, lowers, scales = [], [], []
+    drives[half // 2] += left_drives[half // 2] + right_drives[half // 2]
+
+    states, scales = [], []
+    row_low = lax.broadcasted_iota(jnp.int32, (1, pair), 1) < members
     for total in grams:
         squares = jnp.sum(total * total, axis=0, keepdims=True)
-        row_low = lax.broadcasted_iota(jnp.int32, (1, pair), 1) < members
         sum_low = jnp.sum(jnp.where(row_low, squares, 0.0), axis=1, keepdims=True)
         sum_high = jnp.sum(jnp.where(row_low, 0.0, squares), axis=1, keepdims=True)
         scale = jnp.sqrt(jnp.where(row_low, sum_low, sum_high))
         scales.append(scale)
-        uppers.append(total / scale)
-
+        states.append(total / scale)
+    drives = [jnp.broadcast_to(drive, (THIN, pair)) for drive in drives]
+
+    lowers = []
     for sweep in range(NS_ITERS):
-        if sweep == 0:
-            middles = [1.5 * eye - 0.5 * up for up in uppers]
-            lowers = middles
-            uppers = [times(up, blocks(mid)) for up, mid in zip(uppers, middles)]
-        else:
-            middles = [
-                1.5 * eye - 0.5 * times(lo, blocks(up)) for lo, up in zip(lowers, uppers)
-            ]
-            if sweep < NS_ITERS - 1:
-                both = [
-                    times(jnp.concatenate([up, lo], axis=0), blocks(mid))
-                    for up, lo, mid in zip(uppers, lowers, middles)
-                ]
-                uppers = [x[0:members] for x in both]
-                lowers = [x[members:] for x in both]
-            else:
-                lowers = [times(lo, blocks(mid)) for lo, mid in zip(lowers, middles)]
+        middles = [1.5 * eye - 0.5 * state for state in states]
+        weights = [blocks(mid) for mid in middles]
+        final = sweep == NS_ITERS - 1
+        lefts = [
+            ([] if final else [states[i]]) + ([lowers[i]] if sweep else []) + [drives[i]]
+            for i in range(count)
+        ]
+        once = [times(jnp.concatenate(left, axis=0), w) for left, w in zip(lefts, weights)]
+        lowers = [x[-THIN - members : -THIN] for x in once] if sweep else middles
+        again = [
+            x[-THIN:] if final else jnp.concatenate([x[0:members], x[-THIN:]], axis=0)
+            for x in once
+        ]
+        twice = [times(left, w) for left, w in zip(again, weights)]
+        states = [x[0:members] for x in twice]
+        drives = [x[-THIN:] for x in twice]
+
+    def centered(x):
+        sum_low = jnp.sum(jnp.where(low[0:1], x, 0.0), axis=1, keepdims=True)
+        sum_high = jnp.sum(jnp.where(low[0:1], 0.0, x), axis=1, keepdims=True)
+        return x - jnp.where(low[0:1], sum_low, sum_high) / members
 
     results = []
     for i in range(count):
         root = lowers[i] / jnp.sqrt(scales[i])
-        top = jnp.where(low, drives[2 * i], 0.0)
-        bottom = jnp.where(low, 0.0, drives[2 * i + 1])
-        hi, lo = halves(jnp.concatenate([top, bottom], axis=0))
-        inner = times(root, stationary(hi, lo))
-        shift = times(root, blocks(inner))
+        shift = drives[i][0:1] / scales[i]
         full = math.sqrt(members - 1.0) * root + shift
-        results.append(full - jnp.mean(full, axis=0, keepdims=True) + 1.0 / members)
+        results.append(centered(full) + 1.0 / members)
     for i in range(count):
         mine[i] = results[i]
         product[i] = results[i]
@@ -425,9 +427,11 @@
         def _(step=step):
             lag_copy(step).wait_recv()
             for i in range(count):
-                product[i] = times(product[i], blocks(theirs[step - 1, i]))
+                product[i] = times(theirs[step - 1, i], blocks(product[i]))
     for i in range(count):
-        turned[i * pair : (i + 1) * pair] = product[i].T.astype(BF16)
+        both = product[i].astype(BF16)
+        turned[i * pair : i * pair + members] = both[:, 0:members]
+        turned[i * pair + members : (i + 1) * pair] = both[:, members:]
     ens_load.wait()
 
     for step in range(1, tiles):
@@ -487,7 +491,8 @@
     count = (points + 2) // 2
     pair = 2 * members
     rows = members + META
-    side = (members * (half // 4) + members // 2, pair)
+    vectors = half // 2 + 1 + half // 4
+    side = (members * (half // 4) + members // 2 + -(-vectors // 8) * 8, pair)
     turned, held = pl.pallas_call(
         functools.partial(weights_kernel, tiles, lags, slots, group, columns),
         out_shape=(pltpu.VMEM((count * pair, members), BF16), pltpu.VMEM((members, columns), BF16)),
@@ -504,7 +509,7 @@
             pltpu.VMEM((rows, own), BF16),
             pltpu.VMEM((tiles, rows, slots), BF16),
             pltpu.VMEM((tiles, rows, slots), BF16),
-            pltpu.VMEM((points + 2 * half, members, rows), F32),
+            pltpu.VMEM((points + 2 * half, rows, members), F32),
             pltpu.VMEM(side, F32),
             pltpu.VMEM(side, F32),
             pltpu.VMEM(side, F32),
@@ -520,7 +525,7 @@
             pltpu.VMEM((count, members, pair), F32),
             pltpu.VMEM((rows, slots), BF16),
             pltpu.VMEM((tiles, rows, slots), BF16),
-            pltpu.VMEM((half + 1, members, rows), F32),
+            pltpu.VMEM((half + 1, rows, members), F32),
             pltpu.SemaphoreType.DMA((1,)),
             pltpu.SemaphoreType.DMA((tiles,)),
             pltpu.SemaphoreType.REGULAR((tiles,)),

time: 24 us -> 23.5 us (0.979)
  Pallas kernels: 22.9 us -> 22.4 us
    pallas_call x1, Pallas kernels: 21.8 us -> 21.3 us  [per_device(): pl.pallas_call(functools.partial(weights_kernel, tiles, lags, slots, grou...]
where the time goes in v3:
time: 23.5 us; the launch traced here: 23.1 us
  Pallas kernels  22.4 us (95%)
  between operations  0.66 us (3%)
    pallas_call x1, Pallas kernels, per_device(): pl.pallas_call(functools.partial(weights_kernel, tiles, lags, slots, grou...  21.3 us
    pallas_call x1, Pallas kernels, per_device(): pl.pallas_call(apply_kernel, out_shape=jax.ShapeDtypeStruct((members, col...  1.12 us

profile of v3, /device:TPU:0, one launch (start us, length us, event | category | flops | bytes accessed | tf_op | source)
XLA Modules:
  0.0 23.1 jit_solution(2287204656107019253)
XLA Ops:
  0.7 21.3 %ensemble_weights.1 = (bf16[640,64]{1,0:T(8,128)(2,1)S(1)}, bf16[64,4096]{1,0:T(8,128)(2,1)S(1)}) custom-call(bf16[64,1024]{1,0:T(8,128)(2,1)} %bitcast.5, bf16[1,1024]{1,0:T(2,128)(2,1)} %innov_hbm.1, bf16[1,1024]{1,0:T(2,128)(2,1)} %rinv_hbm.1, s32[1,1024]{1,0:T(1,128)} %bitcast.6, s32[1,1024]{1,0:T(1,128)} %col_hbm.1, s32[1,1]{1,0:T(1,128)S(6)} %copy.8.count_hbm, ...), custom_call_target="tpu_custom_call" | custom-call | tf_op jit(solution)/shard_map/ensemble_weights/pallas_call | solution.py:496
  22.0 1.1 %apply_weights.1 = bf16[64,4096]{1,0:T(8,128)(2,1)} custom-call(bf16[640,64]{1,0:T(8,128)(2,1)S(1)} %get-tuple-element.7.turned, bf16[64,4096]{1,0:T(8,128)(2,1)S(1)} %get-tuple-element.8.ens), custom_call_target="tpu_custom_call" | custom-call | tf_op jit(solution)/shard_map/apply_weights/pallas_call | solution.py:543

commit v4 on v3

--- a/solution.py
+++ b/solution.py
@@ -11,7 +11,6 @@
 SPACING = 512
 NS_ITERS = 6
 THIN = 16
-BATCHES = [2, 2]
 BLOCKS = 4
 LIMIT = 24 * 1024 * 1024
 LANES = 128
@@ -48,6 +47,11 @@
             other = other + bit - 2 * bit * lax.rem(lax.div(me, bit), 2)
         bit *= 2
     return other
+
+
+def batches_of(tiles):
+    starts = [n for n in (0, 2) if n < tiles] + list(range(4, tiles, 4))
+    return [range(a, b) for a, b in zip(starts, starts[1:] + [tiles])]
 
 
 def weights_kernel(
@@ -68,33 +72,6 @@
     me = lax.axis_index("space")
     my_lag = lax.axis_index("lag")
 
-    barrier = pltpu.get_barrier_semaphore()
-    blocks_of = BLOCKS if tiles % BLOCKS == 0 else 1
-    wide = tiles // blocks_of
-    mine_block, inner = lax.div(me, wide), lax.rem(me, wide)
-
-    def rank_of(tile):
-        block, place = lax.div(tile, wide), lax.rem(tile, wide)
-        digits, bit = block, 1
-        while bit < wide:
-            digits = digits + lax.rem(lax.div(place, bit), 2)
-            bit *= 2
-        return digits * tiles + tile
-
-    def before(a, b):
-        return lax.div(b - a + span - 1, span)
-
-    span = tiles * (tiles + blocks_of)
-    my_rank = rank_of(me)
-    ranks_of = [rank_of(jnp.int32(tile)) for tile in range(tiles)]
-    earlier = sum(before(r, my_rank) for r in ranks_of)
-    for peer in range(tiles - 1, -1, -1):
-        @pl.when(my_rank < ranks_of[peer])
-        def _(peer=peer):
-            pl.semaphore_signal(barrier, inc=1, device_id={"space": peer})
-    for step in range(1, lags):
-        pl.semaphore_signal(barrier, inc=1, device_id={"lag": lax.rem(my_lag + step, lags)})
-
     loads = [
         pltpu.make_async_copy(source, dest, load_sem.at[n])
         for n, (source, dest) in enumerate((
@@ -108,6 +85,34 @@
     ]
     for load in loads:
         load.start()
+    barrier = pltpu.get_barrier_semaphore()
+    batches = batches_of(tiles)
+    blocks_of = BLOCKS if tiles % BLOCKS == 0 else 1
+    wide = tiles // blocks_of
+    mine_block, inner = lax.div(me, wide), lax.rem(me, wide)
+
+    def rank_of(tile):
+        block, place = lax.div(tile, wide), lax.rem(tile, wide)
+        digits, bit = block, 1
+        while bit < wide:
+            digits = digits + lax.rem(lax.div(place, bit), 2)
+            bit *= 2
+        return digits * tiles + tile
+
+    def before(a, b):
+        return lax.div(b - a + span - 1, span)
+
+    span = tiles * (tiles + blocks_of)
+    my_rank = rank_of(me)
+    ranks_of = [rank_of(jnp.int32(tile)) for tile in range(tiles)]
+    earlier = sum(before(r, my_rank) for r in ranks_of)
+    for peer in range(tiles - 1, -1, -1):
+        @pl.when(my_rank < ranks_of[peer])
+        def _(peer=peer):
+            pl.semaphore_signal(barrier, inc=1, device_id={"space": peer})
+    for step in range(1, lags):
+        pl.semaphore_signal(barrier, inc=1, device_id={"lag": lax.rem(my_lag + step, lags)})
+
     for load in loads:
         load.wait()
 
@@ -146,60 +151,70 @@
         chosen = jnp.where(place == wanted, jnp.ones((), BF16), jnp.zeros((), BF16))
         return lax.dot_general(message, chosen, NT, preferred_element_type=F32).astype(BF16)
 
-    def a2a(step, peer=None):
+    def a2a(peer):
         return pltpu.make_async_remote_copy(
-            src_ref=snd.at[step, 0:sent], dst_ref=rcv.at[step, 0:sent],
-            send_sem=a2a_send.at[step], recv_sem=a2a_recv.at[step],
-            device_id={"space": me if peer is None else peer},
+            src_ref=snd.at[peer, 0:sent], dst_ref=rcv.at[step_of(peer), 0:sent],
+            send_sem=a2a_send.at[0], recv_sem=a2a_recv.at[lax.div(step_of(peer), group)],
+            device_id={"space": jnp.int32(peer)},
         )
 
     pl.semaphore_wait(barrier, earlier + lags - 1)
+    my_batch = sum(lax.div(me + tiles - batch[0], tiles) for batch in batches[1:])
     for peer in range(tiles):
         @pl.when(ranks_of[peer] < my_rank)
         def _(peer=peer):
-            pl.semaphore_signal(ready.at[me], inc=1, device_id={"space": peer})
+            pl.semaphore_signal(ready.at[my_batch], inc=1, device_id={"space": peer})
 
     def edge_copy(source):
         return pltpu.make_async_remote_copy(
             src_ref=edge.at[0:sent], dst_ref=edge_rcv.at[source, 0:sent],
-            send_sem=edge_send.at[0], recv_sem=edge_recv.at[source],
+            send_sem=edge_send.at[0], recv_sem=edge_recv.at[lax.div(source, group)],
             device_id={"space": 0 * me},
         )
 
     def step_of(peer):
         block, place = peer // wide, peer % wide
-        ahead = lax.rem(mine_block + blocks_of - block, blocks_of)
-        return ahead * wide + partner(inner, place, wide)
+        if blocks_of == 4:
+            across = lax.div(mine_block, 2) - block // 2
+            beside = mine_block - block
+            middle = lax.div(mine_block * (3 - mine_block), 2)
+            turn = (1 - across * across) * beside * beside + across * across * (2 + middle)
+        else:
+            turn = lax.rem(mine_block + blocks_of - block, blocks_of)
+        return turn * wide + partner(inner, place, wide)
 
     def send(peer):
-        @pl.when(my_rank < ranks_of[peer])
-        def _():
-            pl.semaphore_wait(ready.at[peer], 1)
-
         @pl.when(me != peer)
         def _():
-            a2a(step_of(peer), jnp.int32(peer)).start()
-
-    done = 0
-    for size in BATCHES + [4] * tiles:
-        batch = range(done, min(done + size, tiles))
+            a2a(peer).start()
+
+    for n, batch in enumerate(batches):
         for peer in batch:
-            snd[step_of(peer)] = bucket(peer)
-        if done == 0:
+            snd[peer] = bucket(peer)
+        if n == 0:
             edge[...] = bucket(tiles - 1)
+        later = sum(before(my_rank, ranks_of[peer]) for peer in batch)
+
+        @pl.when(later > 0)
+        def _(n=n, later=later):
+            pl.semaphore_wait(ready.at[n], later)
+
         for peer in batch:
             send(peer)
-        if done == 0:
+        if n == 0:
             @pl.when(me > 0)
             def _():
-                edge_copy(me).start()
-        done += size
+                edge_copy(step_of(0)).start()
     for step in range(1, tiles):
         rcv[step, sent:] = jnp.zeros((members + META - sent, slots), BF16)
 
     ens_load = pltpu.make_async_copy(ens_hbm, ens, move_sem.at[0])
     ens_load.start()
     arrivals = list(range(tiles))
+
+    def landed(place, sem, first):
+        part = place.at[max(first, 1) : first + group, 0:sent]
+        return pltpu.make_async_copy(part, part, sem.at[first // group])
 
     def partials(obs, ks, into, base, fresh):
         pert = obs[0:members].astype(F32)
@@ -218,10 +233,9 @@
                 into[k - base] += part
 
     for first in range(0, tiles, group):
-        for step in arrivals[max(first, 1) : first + group]:
-            a2a(step).wait_recv()
+        landed(rcv, a2a_recv, first).wait()
         obs = jnp.concatenate(
-            [rcv[step] if step else snd[0] for step in arrivals[first : first + group]], axis=1
+            [rcv[step] if step else snd[me] for step in arrivals[first : first + group]], axis=1
         )
 
         def moments(ks, obs=obs, first=first):
@@ -229,8 +243,7 @@
 
         @pl.when(me == 0)
         def _(first=first):
-            for step in arrivals[max(first, 1) : first + group]:
-                edge_copy(step).wait_recv()
+            landed(edge_rcv, edge_recv, first).wait()
             near = [
                 edge_rcv[step] if step else edge[...] for step in arrivals[first : first + group]
             ]
@@ -434,8 +447,8 @@
         turned[i * pair + members : (i + 1) * pair] = both[:, members:]
     ens_load.wait()
 
-    for step in range(1, tiles):
-        a2a(step).wait_send()
+    gone = snd.at[1:tiles, 0:sent]
+    pltpu.make_async_copy(gone, gone, a2a_send.at[0]).wait()
     left_copy.wait_send()
 
     @pl.when(me < tiles - 1)
@@ -444,7 +457,7 @@
 
     @pl.when(me > 0)
     def _():
-        edge_copy(me).wait_send()
+        edge_copy(step_of(0)).wait_send()
 
     for step in range(1, lags):
         @pl.when(my_lag >= step)
@@ -516,8 +529,8 @@
             pltpu.VMEM(side, F32),
             pltpu.VMEM((count, members, pair), F32),
             pltpu.VMEM((max(lags - 1, 1), count, members, pair), F32),
-            pltpu.SemaphoreType.DMA((tiles,)),
-            pltpu.SemaphoreType.DMA((tiles,)),
+            pltpu.SemaphoreType.DMA((1,)),
+            pltpu.SemaphoreType.DMA((-(-tiles // group),)),
             pltpu.SemaphoreType.DMA((2,)),
             pltpu.SemaphoreType.DMA((2,)),
             pltpu.SemaphoreType.DMA((max(lags - 1, 1),)),
@@ -527,8 +540,8 @@
             pltpu.VMEM((tiles, rows, slots), BF16),
             pltpu.VMEM((half + 1, rows, members), F32),
             pltpu.SemaphoreType.DMA((1,)),
-            pltpu.SemaphoreType.DMA((tiles,)),
-            pltpu.SemaphoreType.REGULAR((tiles,)),
+            pltpu.SemaphoreType.DMA((-(-tiles // group),)),
+            pltpu.SemaphoreType.REGULAR((len(batches_of(tiles)),)),
         ],
         compiler_params=pltpu.CompilerParams(
             collective_id=0, has_side_effects=True, vmem_limit_bytes=LIMIT

time: 23.5 us -> 22.4 us (0.953)
  Pallas kernels: 22.4 us -> 21.4 us
    pallas_call x1, Pallas kernels: 21.3 us -> 20.3 us  [per_device(): pl.pallas_call(functools.partial(weights_kernel, tiles, lags, slots, grou...]
where the time goes in v4:
time: 22.4 us; the launch traced here: 22.1 us
  Pallas kernels  21.4 us (96%)
  between operations  0.66 us (3%)
    pallas_call x1, Pallas kernels, per_device(): pl.pallas_call(functools.partial(weights_kernel, tiles, lags, slots, grou...  20.3 us
    pallas_call x1, Pallas kernels, per_device(): pl.pallas_call(apply_kernel, out_shape=jax.ShapeDtypeStruct((members, col...  1.11 us

profile of v4, /device:TPU:0, one launch (start us, length us, event | category | flops | bytes accessed | tf_op | source)
XLA Modules:
  0.0 22.1 jit_solution(1826650394011060129)
XLA Ops:
  0.7 20.3 %ensemble_weights.1 = (bf16[640,64]{1,0:T(8,128)(2,1)S(1)}, bf16[64,4096]{1,0:T(8,128)(2,1)S(1)}) custom-call(bf16[64,1024]{1,0:T(8,128)(2,1)} %bitcast.5, bf16[1,1024]{1,0:T(2,128)(2,1)} %innov_hbm.1, bf16[1,1024]{1,0:T(2,128)(2,1)} %rinv_hbm.1, s32[1,1024]{1,0:T(1,128)} %bitcast.6, s32[1,1024]{1,0:T(1,128)} %col_hbm.1, s32[1,1]{1,0:T(1,128)S(6)} %copy.8.count_hbm, ...), custom_call_target="tpu_custom_call" | custom-call | tf_op jit(solution)/shard_map/ensemble_weights/pallas_call | solution.py:509
  21.0 1.1 %apply_weights.1 = bf16[64,4096]{1,0:T(8,128)(2,1)} custom-call(bf16[640,64]{1,0:T(8,128)(2,1)S(1)} %get-tuple-element.7.turned, bf16[64,4096]{1,0:T(8,128)(2,1)S(1)} %get-tuple-element.8.ens), custom_call_target="tpu_custom_call" | custom-call | tf_op jit(solution)/shard_map/apply_weights/pallas_call | solution.py:556

commit v5 on v4

--- a/solution.py
+++ b/solution.py
@@ -38,15 +38,15 @@
     return out[:, :width] + out[:, width:]
 
 
-def partner(me, step, tiles):
-    if tiles & (tiles - 1):
-        return lax.rem(me + tiles - step, tiles)
-    other, bit = me, 1
-    while bit < tiles:
-        if step & bit:
-            other = other + bit - 2 * bit * lax.rem(lax.div(me, bit), 2)
+def mixed(a, b, width):
+    if width & (width - 1):
+        return lax.rem(a + width - b, width)
+    out, bit = 0, 1
+    while bit < width:
+        one, two = lax.rem(lax.div(a, bit), 2), lax.rem(lax.div(b, bit), 2)
+        out = out + bit * (one + two - 2 * one * two)
         bit *= 2
-    return other
+    return out
 
 
 def batches_of(tiles):
@@ -60,7 +60,7 @@
     turned, ens,
     move_sem,
     innov_ref, rinv_ref, tile_ref, col_ref, count_ref, load_sem,
-    msg, snd, rcv, acc, to_left, to_right, from_left, from_right, mine, theirs,
+    msg, snd, rcv, snd_meta, rcv_meta, acc, to_left, to_right, from_left, from_right, mine, theirs,
     a2a_send, a2a_recv, halo_send, halo_recv, lag_send, lag_recv, product, edge, edge_rcv, edge_acc, edge_send, edge_recv, ready,
 ):
     members, own = pert_hbm.shape
@@ -87,7 +87,7 @@
         load.start()
     barrier = pltpu.get_barrier_semaphore()
     batches = batches_of(tiles)
-    blocks_of = BLOCKS if tiles % BLOCKS == 0 else 1
+    blocks_of = BLOCKS
     wide = tiles // blocks_of
     mine_block, inner = lax.div(me, wide), lax.rem(me, wide)
 
@@ -152,11 +152,15 @@
         return lax.dot_general(message, chosen, NT, preferred_element_type=F32).astype(BF16)
 
     def a2a(peer):
-        return pltpu.make_async_remote_copy(
-            src_ref=snd.at[peer, 0:sent], dst_ref=rcv.at[step_of(peer), 0:sent],
-            send_sem=a2a_send.at[0], recv_sem=a2a_recv.at[lax.div(step_of(peer), group)],
-            device_id={"space": jnp.int32(peer)},
-        )
+        step = step_of(peer)
+        return [
+            pltpu.make_async_remote_copy(
+                src_ref=source.at[peer], dst_ref=dest.at[step],
+                send_sem=a2a_send.at[n], recv_sem=a2a_recv.at[n, lax.div(step, group)],
+                device_id={"space": peer},
+            )
+            for n, (source, dest) in enumerate(((snd, rcv), (snd_meta, rcv_meta)))
+        ]
 
     pl.semaphore_wait(barrier, earlier + lags - 1)
     my_batch = sum(lax.div(me + tiles - batch[0], tiles) for batch in batches[1:])
@@ -173,48 +177,59 @@
         )
 
     def step_of(peer):
-        block, place = peer // wide, peer % wide
-        if blocks_of == 4:
-            across = lax.div(mine_block, 2) - block // 2
-            beside = mine_block - block
-            middle = lax.div(mine_block * (3 - mine_block), 2)
-            turn = (1 - across * across) * beside * beside + across * across * (2 + middle)
-        else:
-            turn = lax.rem(mine_block + blocks_of - block, blocks_of)
-        return turn * wide + partner(inner, place, wide)
+        block, place = lax.div(peer, wide), lax.rem(peer, wide)
+        across = lax.div(mine_block, 2) - lax.div(block, 2)
+        beside = mine_block - block
+        middle = lax.div(mine_block * (3 - mine_block), 2)
+        turn = (1 - across * across) * beside * beside + across * across * (2 + middle)
+        return turn * wide + mixed(inner, place, wide)
 
     def send(peer):
         @pl.when(me != peer)
         def _():
-            a2a(peer).start()
-
+            for copy in a2a(peer):
+                copy.start()
+
+    lower = 1 - lax.div(mine_block, 2)
+    fills, plans = [], []
     for n, batch in enumerate(batches):
-        for peer in batch:
-            snd[peer] = bucket(peer)
-        if n == 0:
-            edge[...] = bucket(tiles - 1)
-        later = sum(before(my_rank, ranks_of[peer]) for peer in batch)
+        block = batch[0] // wide
+        shift = (1 - lower) * (4 - 2 * block) * wide if block % 2 else jnp.int32(0)
+        peers = [jnp.int32(tile) + shift for tile in batch]
+        def fill(n=n, peers=peers):
+            for peer in peers:
+                filled = bucket(peer)
+                snd[peer] = filled[0:members]
+                snd_meta[peer] = filled[members : members + META // 4]
+            if n == len(batches) - 1:
+                edge[...] = bucket(tiles - 1)
+
+        fills.append(fill)
+        plans.append((peers, shift))
+    fills[0]()
+    pl.when(mine_block == 0)(lambda: [fill() for fill in fills[1:]] and None)
+    for n, (peers, shift) in enumerate(plans):
+        if n:
+            pl.when(mine_block > 0)(fills[n])
+        later = sum(before(my_rank, rank_of(peer)) for peer in peers)
 
         @pl.when(later > 0)
-        def _(n=n, later=later):
-            pl.semaphore_wait(ready.at[n], later)
-
-        for peer in batch:
+        def _(n=n, later=later, shift=shift):
+            pl.semaphore_wait(ready.at[n + lax.div(shift, 4)], later)
+
+        for peer in peers:
             send(peer)
-        if n == 0:
+        if n == len(batches) - 1:
             @pl.when(me > 0)
             def _():
-                edge_copy(step_of(0)).start()
-    for step in range(1, tiles):
-        rcv[step, sent:] = jnp.zeros((members + META - sent, slots), BF16)
-
+                edge_copy(step_of(me * 0)).start()
     ens_load = pltpu.make_async_copy(ens_hbm, ens, move_sem.at[0])
     ens_load.start()
     arrivals = list(range(tiles))
 
     def landed(place, sem, first):
-        part = place.at[max(first, 1) : first + group, 0:sent]
-        return pltpu.make_async_copy(part, part, sem.at[first // group])
+        part = place.at[max(first, 1) : first + group]
+        return pltpu.make_async_copy(part, part, sem)
 
     def partials(obs, ks, into, base, fresh):
         pert = obs[0:members].astype(F32)
@@ -233,24 +248,22 @@
                 into[k - base] += part
 
     for first in range(0, tiles, group):
-        landed(rcv, a2a_recv, first).wait()
+        landed(rcv, a2a_recv.at[0, first // group], first).wait()
+        landed(rcv_meta, a2a_recv.at[1, first // group], first).wait()
+        steps = arrivals[first : first + group]
         obs = jnp.concatenate(
-            [rcv[step] if step else snd[me] for step in arrivals[first : first + group]], axis=1
+            [
+                jnp.concatenate([rcv[step] if step else snd[me] for step in steps], axis=1),
+                jnp.concatenate(
+                    [rcv_meta[step] if step else snd_meta[me] for step in steps], axis=1
+                ),
+                jnp.zeros((META - META // 4, group * slots), BF16),
+            ],
+            axis=0,
         )
 
         def moments(ks, obs=obs, first=first):
             partials(obs, ks, acc, 0, first == 0)
-
-        @pl.when(me == 0)
-        def _(first=first):
-            landed(edge_rcv, edge_recv, first).wait()
-            near = [
-                edge_rcv[step] if step else edge[...] for step in arrivals[first : first + group]
-            ]
-            partials(
-                jnp.concatenate(near, axis=1), range(points + half - 1, points + 2 * half),
-                edge_acc, points + half - 1, first == 0,
-            )
 
         if first + group < tiles:
             moments(range(points + 2 * half))
@@ -348,15 +361,24 @@
     count = (points + 2) // 2
     own_pairs = [joined(half - 1 + 2 * i, half + 2 * i) for i in range(count)]
     own_drives = [drives_of(half - 1 + 2 * i, half + 2 * i) for i in range(count)]
+    @pl.when(me == 0)
+    def _():
+        for first in range(0, tiles, group):
+            landed(edge_rcv.at[:, 0:sent], edge_recv.at[first // group], first).wait()
+            near = [
+                edge_rcv[step] if step else edge[...] for step in arrivals[first : first + group]
+            ]
+            partials(
+                jnp.concatenate(near, axis=1), range(points + half - 1, points + 2 * half),
+                edge_acc, points + half - 1, first == 0,
+            )
+        from_left[...] = packed(half, list(range(half)), edge_acc)
+
     left_copy.wait_recv()
 
     @pl.when(me > 0)
     def _():
         right_copy.wait_recv()
-
-    @pl.when(me == 0)
-    def _():
-        from_left[...] = packed(half, list(range(half)), edge_acc)
 
     lefts, left_single, left_drives = unpacked(from_left)
     rights, right_single, right_drives = unpacked(from_right)
@@ -447,8 +469,9 @@
         turned[i * pair + members : (i + 1) * pair] = both[:, members:]
     ens_load.wait()
 
-    gone = snd.at[1:tiles, 0:sent]
-    pltpu.make_async_copy(gone, gone, a2a_send.at[0]).wait()
+    for n, source in enumerate((snd, snd_meta)):
+        gone = source.at[1:tiles]
+        pltpu.make_async_copy(gone, gone, a2a_send.at[n]).wait()
     left_copy.wait_send()
 
     @pl.when(me < tiles - 1)
@@ -457,7 +480,7 @@
 
     @pl.when(me > 0)
     def _():
-        edge_copy(step_of(0)).wait_send()
+        edge_copy(step_of(me * 0)).wait_send()
 
     for step in range(1, lags):
         @pl.when(my_lag >= step)
@@ -520,8 +543,10 @@
             pltpu.SMEM((1, 1), jnp.int32),
             pltpu.SemaphoreType.DMA((6,)),
             pltpu.VMEM((rows, own), BF16),
-            pltpu.VMEM((tiles, rows, slots), BF16),
-            pltpu.VMEM((tiles, rows, slots), BF16),
+            pltpu.VMEM((tiles, members, slots), BF16),
+            pltpu.VMEM((tiles, members, slots), BF16),
+            pltpu.VMEM((tiles, META // 4, slots), BF16),
+            pltpu.VMEM((tiles, META // 4, slots), BF16),
             pltpu.VMEM((points + 2 * half, rows, members), F32),
             pltpu.VMEM(side, F32),
             pltpu.VMEM(side, F32),
@@ -529,8 +554,8 @@
             pltpu.VMEM(side, F32),
             pltpu.VMEM((count, members, pair), F32),
             pltpu.VMEM((max(lags - 1, 1), count, members, pair), F32),
-            pltpu.SemaphoreType.DMA((1,)),
-            pltpu.SemaphoreType.DMA((-(-tiles // group),)),
+            pltpu.SemaphoreType.DMA((2,)),
+            pltpu.SemaphoreType.DMA((2, -(-tiles // group))),
             pltpu.SemaphoreType.DMA((2,)),
             pltpu.SemaphoreType.DMA((2,)),
             pltpu.SemaphoreType.DMA((max(lags - 1, 1),)),

time: 22.4 us -> 22 us (0.982)
  the two profiles are of different devices: /device:TPU:0 before, /device:TPU:28 now
where the time goes in v5:
time: 22 us; the launch traced here: 21.8 us
  Pallas kernels  21.1 us (96%)
  between operations  0.66 us (3%)
    pallas_call x1, Pallas kernels, per_device(): pl.pallas_call(functools.partial(weights_kernel, tiles, lags, slots, grou...  20 us
    pallas_call x1, Pallas kernels, per_device(): pl.pallas_call(apply_kernel, out_shape=jax.ShapeDtypeStruct((members, col...  1.12 us

profile of v5, /device:TPU:28, one launch (start us, length us, event | category | flops | bytes accessed | tf_op | source)
XLA Modules:
  0.0 21.8 jit_solution(10440385092426332434)
XLA Ops:
  0.7 20.0 %ensemble_weights.1 = (bf16[640,64]{1,0:T(8,128)(2,1)S(1)}, bf16[64,4096]{1,0:T(8,128)(2,1)S(1)}) custom-call(bf16[64,1024]{1,0:T(8,128)(2,1)} %bitcast.5, bf16[1,1024]{1,0:T(2,128)(2,1)} %innov_hbm.1, bf16[1,1024]{1,0:T(2,128)(2,1)} %rinv_hbm.1, s32[1,1024]{1,0:T(1,128)} %bitcast.6, s32[1,1024]{1,0:T(1,128)} %col_hbm.1, s32[1,1]{1,0:T(1,128)S(6)} %copy.8.count_hbm, ...), custom_call_target="tpu_custom_call" | custom-call | tf_op jit(solution)/shard_map/ensemble_weights/pallas_call | solution.py:532
  20.7 1.1 %apply_weights.1 = bf16[64,4096]{1,0:T(8,128)(2,1)} custom-call(bf16[640,64]{1,0:T(8,128)(2,1)S(1)} %get-tuple-element.7.turned, bf16[64,4096]{1,0:T(8,128)(2,1)S(1)} %get-tuple-element.8.ens), custom_call_target="tpu_custom_call" | custom-call | tf_op jit(solution)/shard_map/apply_weights/pallas_call | solution.py:581

commit v6 on v5

--- a/solution.py
+++ b/solution.py
@@ -10,6 +10,7 @@
 
 SPACING = 512
 NS_ITERS = 6
+TAIL = 2
 THIN = 16
 BLOCKS = 4
 LIMIT = 24 * 1024 * 1024
@@ -113,20 +114,7 @@
     for step in range(1, lags):
         pl.semaphore_signal(barrier, inc=1, device_id={"lag": lax.rem(my_lag + step, lags)})
 
-    for load in loads:
-        load.wait()
-
-    slot_id = lax.broadcasted_iota(jnp.int32, (1, own), 1)
-    weight = jnp.where(slot_id < count_ref[0, 0], rinv_ref[...].astype(F32), 0.0)
-    column = col_ref[...]
-    col_hi = (column // BASE).astype(F32)
-    col_lo = (column % BASE).astype(F32)
-    row = lax.broadcasted_iota(jnp.int32, (META, own), 0)
-    meta = jnp.where(row == 0, weight, 0.0)
-    meta = jnp.where(row == 1, innov_ref[...].astype(F32), meta)
-    meta = jnp.where(row == 2, col_hi, meta)
-    meta = jnp.where(row == 3, col_lo, meta)
-    msg[members:, :] = meta.astype(BF16)
+    loads[0].wait()
 
     target = tile_ref[...]
     hits = jnp.where(target == lax.broadcasted_iota(jnp.int32, (tiles, own), 0), 1.0, 0.0)
@@ -144,7 +132,6 @@
         seen = seen + jnp.sum(block, axis=1, keepdims=True)
     rank = jnp.concatenate(ranks, axis=1)
     place = lax.broadcasted_iota(jnp.int32, (slots, own), 0).astype(F32).astype(BF16)
-    message = msg[...]
 
     def bucket(dest):
         wanted = jnp.where(target == dest, rank, -1.0).astype(BF16)
@@ -156,7 +143,7 @@
         return [
             pltpu.make_async_remote_copy(
                 src_ref=source.at[peer], dst_ref=dest.at[step],
-                send_sem=a2a_send.at[n], recv_sem=a2a_recv.at[n, lax.div(step, group)],
+                send_sem=a2a_send.at[n], recv_sem=a2a_recv.at[n, lax.div(step, group) + lax.div(step, tiles - TAIL)],
                 device_id={"space": peer},
             )
             for n, (source, dest) in enumerate(((snd, rcv), (snd_meta, rcv_meta)))
@@ -190,6 +177,21 @@
             for copy in a2a(peer):
                 copy.start()
 
+    for load in loads[1:]:
+        load.wait()
+    slot_id = lax.broadcasted_iota(jnp.int32, (1, own), 1)
+    weight = jnp.where(slot_id < count_ref[0, 0], rinv_ref[...].astype(F32), 0.0)
+    column = col_ref[...]
+    col_hi = (column // BASE).astype(F32)
+    col_lo = (column % BASE).astype(F32)
+    row = lax.broadcasted_iota(jnp.int32, (META, own), 0)
+    meta = jnp.where(row == 0, weight, 0.0)
+    meta = jnp.where(row == 1, innov_ref[...].astype(F32), meta)
+    meta = jnp.where(row == 2, col_hi, meta)
+    meta = jnp.where(row == 3, col_lo, meta)
+    msg[members:, :] = meta.astype(BF16)
+
+    message = msg[...]
     lower = 1 - lax.div(mine_block, 2)
     fills, plans = [], []
     for n, batch in enumerate(batches):
@@ -227,8 +229,8 @@
     ens_load.start()
     arrivals = list(range(tiles))
 
-    def landed(place, sem, first):
-        part = place.at[max(first, 1) : first + group]
+    def landed(place, sem, first, size):
+        part = place.at[max(first, 1) : first + size]
         return pltpu.make_async_copy(part, part, sem)
 
     def partials(obs, ks, into, base, fresh):
@@ -247,17 +249,18 @@
             else:
                 into[k - base] += part
 
-    for first in range(0, tiles, group):
-        landed(rcv, a2a_recv.at[0, first // group], first).wait()
-        landed(rcv_meta, a2a_recv.at[1, first // group], first).wait()
-        steps = arrivals[first : first + group]
+    starts = [*range(0, tiles, group), tiles - TAIL]
+    for turn, (first, size) in enumerate(zip(starts, [group] * (tiles // group - 1) + [group - TAIL, TAIL])):
+        landed(rcv, a2a_recv.at[0, turn], first, size).wait()
+        landed(rcv_meta, a2a_recv.at[1, turn], first, size).wait()
+        steps = arrivals[first : first + size]
         obs = jnp.concatenate(
             [
                 jnp.concatenate([rcv[step] if step else snd[me] for step in steps], axis=1),
                 jnp.concatenate(
                     [rcv_meta[step] if step else snd_meta[me] for step in steps], axis=1
                 ),
-                jnp.zeros((META - META // 4, group * slots), BF16),
+                jnp.zeros((META - META // 4, size * slots), BF16),
             ],
             axis=0,
         )
@@ -265,7 +268,7 @@
         def moments(ks, obs=obs, first=first):
             partials(obs, ks, acc, 0, first == 0)
 
-        if first + group < tiles:
+        if first + size < tiles:
             moments(range(points + 2 * half))
 
     lane = lax.broadcasted_iota(jnp.int32, (members, pair), 1)
@@ -364,7 +367,7 @@
     @pl.when(me == 0)
     def _():
         for first in range(0, tiles, group):
-            landed(edge_rcv.at[:, 0:sent], edge_recv.at[first // group], first).wait()
+            landed(edge_rcv.at[:, 0:sent], edge_recv.at[first // group], first, group).wait()
             near = [
                 edge_rcv[step] if step else edge[...] for step in arrivals[first : first + group]
             ]
@@ -555,7 +558,7 @@
             pltpu.VMEM((count, members, pair), F32),
             pltpu.VMEM((max(lags - 1, 1), count, members, pair), F32),
             pltpu.SemaphoreType.DMA((2,)),
-            pltpu.SemaphoreType.DMA((2, -(-tiles // group))),
+            pltpu.SemaphoreType.DMA((2, tiles // group + 1)),
             pltpu.SemaphoreType.DMA((2,)),
             pltpu.SemaphoreType.DMA((2,)),
             pltpu.SemaphoreType.DMA((max(lags - 1, 1),)),

time: 22 us -> 22 us (level)
  no operation moved by 1% of the time
where the time goes in v6:
time: 22 us; the launch traced here: 21.8 us
  Pallas kernels  21.1 us (96%)
  between operations  0.66 us (3%)
    pallas_call x1, Pallas kernels, per_device(): pl.pallas_call(functools.partial(weights_kernel, tiles, lags, slots, grou...  20 us
    pallas_call x1, Pallas kernels, per_device(): pl.pallas_call(apply_kernel, out_shape=jax.ShapeDtypeStruct((members, col...  1.12 us

profile of v6, /device:TPU:28, one launch (start us, length us, event | category | flops | bytes accessed | tf_op | source)
XLA Modules:
  0.0 21.8 jit_solution(11433796275439753714)
XLA Ops:
  0.7 20.0 %ensemble_weights.1 = (bf16[640,64]{1,0:T(8,128)(2,1)S(1)}, bf16[64,4096]{1,0:T(8,128)(2,1)S(1)}) custom-call(bf16[64,1024]{1,0:T(8,128)(2,1)} %bitcast.5, bf16[1,1024]{1,0:T(2,128)(2,1)} %innov_hbm.1, bf16[1,1024]{1,0:T(2,128)(2,1)} %rinv_hbm.1, s32[1,1024]{1,0:T(1,128)} %bitcast.6, s32[1,1024]{1,0:T(1,128)} %col_hbm.1, s32[1,1]{1,0:T(1,128)S(6)} %copy.8.count_hbm, ...), custom_call_target="tpu_custom_call" | custom-call | tf_op jit(solution)/shard_map/ensemble_weights/pallas_call | solution.py:535
  20.7 1.1 %apply_weights.1 = bf16[64,4096]{1,0:T(8,128)(2,1)} custom-call(bf16[640,64]{1,0:T(8,128)(2,1)S(1)} %get-tuple-element.7.turned, bf16[64,4096]{1,0:T(8,128)(2,1)S(1)} %get-tuple-element.8.ens), custom_call_target="tpu_custom_call" | custom-call | tf_op jit(solution)/shard_map/apply_weights/pallas_call | solution.py:584
